TPU v7x, 32 devices: a whole 2x2x4 slice. The times are simulated.
32 devices in a mesh: groups: 2 (over y), gx: 4 (over z), gy: 4 (over x, core).
Axes of the slice: x: 2, y: 2, z: 4, core: 2. Of those that a mesh axis runs over, the one named last changes fastest.
Arguments:
- tokens: bfloat16 [2, 16, 16384], P(None, 'groups', 'gx'), parts along dimension 1, may hold values from -20 to 20, as said below
- lengths: int32 [2, 16], P(None, ('groups', 'gx')), parts along dimension 1, may hold values from 1 to 1024, as said below
- norm_gain: bfloat16 [16384], P('gx'), may hold values from 0.5 to 2
- w_query: bfloat16 [16384, 8192], P('gx', 'gy'), may hold values from -1.171875 to 1.171875
- key_value_weight: bfloat16 [16384, 4, 256], P('gx', 'gy'), may hold values from -0.046875 to 0.046875
- w_out: bfloat16 [8192, 16384], P('gy', 'gx'), may hold values from -0.0625 to 0.0625
- cache: bfloat16 [2, 16, 1024, 4, 2, 128], P(None, ('groups', 'gx'), None, 'gy'), parts along dimension 1, may hold values from -16 to 16
Outputs:
- layer_out: bfloat16 [2, 16, 16384], P(None, 'groups', 'gx'), parts along dimension 1
There are 2 independent parts, one for each index of `groups`. A program takes and returns all parts, laid end to end along the dimension named above; an argument that names none is the same for every part. Nothing has to cross between parts.
Inputs may be any that keep to these rules, and one draw needn't show every extreme that they name: `tokens`: entries vary with the feature and the row. `lengths`: some rollout has exactly 1024 cached positions in every draw.
All inputs are finite; a program needn't handle non-finite values.
Results may differ from a plain program's by a relative error of at most 0.012.
The roundings to bfloat16 on the way count: a program that leaves them out, or rounds other values in their place, can miss the bound.
Values may be sent and summed in bfloat16 or wider, within the bound.
No kernel may reach another device: no remote copies, remote signals or barrier semaphores. Data moves between devices by JAX's collectives and lax.ppermute only.
A program may use at most 128 MiB of HBM per device.

v0:
```python
import jax
import jax.numpy as jnp
from jax import lax
from jax.sharding import PartitionSpec as P

MODEL_WIDTH = 16384
HEAD_SIZE = 128


def rotate(vectors, positions):
    half = vectors.shape[-1] // 2
    freq = 500000.0 ** (-2.0 * jnp.arange(half, dtype=jnp.float32) / vectors.shape[-1])
    angle = positions[..., None] * freq
    cosine = jnp.cos(angle)
    sine = jnp.sin(angle)
    first = vectors[..., :half]
    second = vectors[..., half:]
    return jnp.concatenate(
        [first * cosine - second * sine, second * cosine + first * sine], axis=-1
    )


def attend(query_sum, keyval_sum, local_squares, lengths, cache):
    batches, rows_here = lengths.shape
    score_scale = lax.rsqrt(local_squares / MODEL_WIDTH + 1e-05)
    heads_kv = keyval_sum.shape[2]
    query_group = query_sum.shape[2] // (heads_kv * HEAD_SIZE)
    query = (
        query_sum.reshape(batches, rows_here, heads_kv, query_group, HEAD_SIZE)
        * score_scale[:, :, None, None, None]
    )
    key_value = keyval_sum * score_scale[:, :, None, None]
    positions = lengths.astype(jnp.float32)
    rotated_query = rotate(query, positions[:, :, None, None]).astype(jnp.bfloat16)
    rkey = rotate(key_value[..., :HEAD_SIZE], positions[:, :, None])
    value_new = key_value[..., HEAD_SIZE:]
    inv_root = 1.0 / jnp.sqrt(jnp.float32(HEAD_SIZE))
    keys = cache[:, :, :, :, 0, :]
    values = cache[:, :, :, :, 1, :]
    scores = (
        jnp.einsum("mrkgd,mrskd->mrkgs", rotated_query, keys, preferred_element_type=jnp.float32)
        * inv_root
    )
    valid = jnp.arange(cache.shape[2], dtype=jnp.int32)[None, None, :] < lengths[:, :, None]
    scores = jnp.where(valid[:, :, None, None, :], scores, -1e30)
    new_score = (
        jnp.sum(rotated_query.astype(jnp.float32) * rkey[:, :, :, None, :], axis=-1) * inv_root
    )
    top = jnp.maximum(jnp.max(scores, axis=-1), new_score)
    weights = jnp.exp(scores - top[..., None])
    new_weight = jnp.exp(new_score - top)
    total = jnp.sum(weights, axis=-1) + new_weight
    summed = jnp.einsum(
        "mrkgs,mrskd->mrkgd",
        weights.astype(jnp.bfloat16),
        values,
        preferred_element_type=jnp.float32,
    )
    summed = summed + new_weight[..., None] * value_new[:, :, :, None, :]
    return (
        (summed / total[..., None])
        .astype(jnp.bfloat16)
        .reshape(batches, rows_here, heads_kv * query_group * HEAD_SIZE)
    )


def local(tokens, lengths, norm_gain, w_query, key_value_weight, w_out, cache):
    x_full = tokens.astype(jnp.float32)
    squares = jnp.sum(x_full * x_full, axis=-1)
    normed = (x_full * norm_gain.astype(jnp.float32)).astype(jnp.bfloat16)
    query_part = jnp.einsum("mrd,dc->mrc", normed, w_query, preferred_element_type=jnp.float32)
    keyval_part = jnp.einsum(
        "mrd,dkc->mrkc", normed, key_value_weight, preferred_element_type=jnp.float32
    )
    query_sum, keyval_sum, local_squares = (
        lax.psum_scatter(query_part, "gx", scatter_dimension=1, tiled=True),
        lax.psum_scatter(keyval_part, "gx", scatter_dimension=1, tiled=True),
        lax.psum_scatter(squares, "gx", scatter_dimension=1, tiled=True),
    )
    attended = attend(query_sum, keyval_sum, local_squares, lengths, cache)
    projected = jnp.einsum(
        "mrc,cd->mrd",
        lax.all_gather(attended, "gx", axis=1, tiled=True),
        w_out,
        preferred_element_type=jnp.float32,
    )
    summed_heads = lax.psum(projected, "gy")
    return (x_full + summed_heads).astype(jnp.bfloat16)


def solution(mesh):
    placed = (
        P(None, "groups", "gx"),
        P(None, ("groups", "gx")),
        P("gx"),
        P("gx", "gy"),
        P("gx", "gy", None),
        P("gy", "gx"),
        P(None, ("groups", "gx"), None, "gy", None, None),
    )
    return jax.shard_map(
        local, mesh=mesh, in_specs=placed, out_specs=P(None, "groups", "gx"), check_vma=False
    )
```

profile of v0, /device:TPU:0, one launch (start us, length us, event | category | flops | bytes accessed | tf_op | source)
XLA Modules:
  0.0 122.0 jit_solution(11372717634072038642)
XLA Ops:
  6.5 0.0 copy-start
  6.5 0.0 all-reduce.9.cloned.1.call-start
  6.5 0.8 convert_element_type.46
  7.4 0.0 copy-start.1
  7.4 0.0 copy-start.2
  7.4 8.8 %fusion.2 = f32[2,8,2048]{2,1,0:T(8,128)} fusion(bf16[4096,2048]{1,0:T(8,128)(2,1)} %param.10, bf16[2,8,4096]{2,1,0:T(8,128)(2,1)} %param.7, f32[4096]{0:T(1024)S(1)} %convert_element_type.46), kind=kOutput, calls=%fused_computation.2 | convolution fusion | flops 268632064 | bytes 17055744 | tf_op jit(solution)/shard_map/mrd,dc->mrc/dot_general | solution.py:71
  16.2 0.0 copy-start.3
  16.2 0.0 all-reduce.9.cloned.1.call-update
  16.2 0.0 all-reduce.7.cloned.1.call-start
  16.3 0.0 copy-done.1
  16.3 0.1 fusion.13
  16.4 0.0 copy-done.2
  16.4 0.1 iota_compare_fusion
  16.5 0.0 copy-done
  16.5 0.4 fusion.9
  16.9 0.0 copy-done.3
  16.9 0.7 dynamic-slice
  18.3 0.1 multiply_cosine_fusion.1
  18.4 20.8 %all-reduce.3 = (f32[2,8]{1,0:T(2,128)S(1)}, f32[2,8,1,256]{3,1,0,2:T(8,128)S(1)}) all-reduce(f32[2,8]{1,0:T(2,128)S(1)} %fusion.13, f32[2,8,1,256]{3,1,0,2:T(8,128)S(1)} %fusion.9), channel_id=3, replica_groups=mesh['groups'=2,'gx'=4,'gy'=4] {'gx'}, use_global_device_ids=true, to_apply=%region_2.0.clone | all-reduce | flops 4112 | bytes 32896
  39.2 0.1 fusion.32
  39.3 0.1 dynamic-slice_multiply_fusion
  39.4 0.1 fusion.29
  39.5 6.9 %fusion.35 = (bf16[2,2,1024,1,1,128]{5,4,3,2,1,0:T(2,128)(2,1)}, bf16[2,2,1024,1,1,128]{5,4,3,2,1,0:T(2,128)(2,1)}) fusion(bf16[2,2,1024,1,2,128]{5,4,3,2,1,0:T(2,128)(2,1)} %param.13), kind=kLoop, calls=%fused_computation.55 | loop fusion | bytes 4194304 | tf_op jit(solution)/shard_map/slice | solution.py:38
  46.4 0.1 maximum_bitcast_fusion
  46.5 7.3 %all-reduce.9.cloned.1.call-done = f32[2,8,2048]{2,1,0:T(8,128)} async-done(((f32[2,8,2048]{2,1,0:T(8,128)}), f32[2,8,2048]{2,1,0:T(8,128)}) %all-reduce.9.cloned.1.call-update) | async-done | bytes 131088
  53.9 0.9 constant_dynamic-slice_fusion
  54.8 0.1 broadcast_multiply_fusion
  54.9 0.1 subtract_convert_fusion
  55.0 0.2 multiply_reduce_fusion
  55.1 2.1 %fusion.36 = (f32[2,2,16]{2,1,0:T(2,128)S(1)}, f32[2,2,16,1024]{3,2,1,0:T(8,128)S(1)}) fusion(bf16[2,2,1024,1,1,128]{5,4,3,2,1,0:T(2,128)(2,1)} %get-tuple-element.9, bf16[2,2,16,64]{3,2,1,0:T(8,128)(2,1)S(1)} %bitcast.38, bf16[2,2,16,64]{3,2,1,0:T(8,128)(2,1)S(1)} %bitcast.37, pred[2,2,1024]{2,1,0:T(4,128)(4,1)S(1)} %iota_compare_fusion), kind=kOutput, calls=%fused_computation.56 | convolution fusion | flops 17006528 | bytes 1331456 | tf_op jit(solution)/shard_map/mrkgd,mrskd->mrkgs/dot_general | solution.py:41
  57.3 0.2 fusion.15
  57.5 1.9 %fusion.8 = bf16[2,2,16,128]{3,2,1,0:T(8,128)(2,1)S(1)} fusion(bf16[2,2,1024,1,1,128]{5,4,3,2,1,0:T(2,128)(2,1)} %get-tuple-element.10, f32[2,2,16,1024]{3,2,1,0:T(8,128)S(1)} %get-tuple-element.18, f32[2,2,16]{2,1,0:T(2,128)S(1)} %multiply_maximum_fusion, f32[2,2,16]{2,1,0:T(2,128)S(1)} %get-tuple-element.7, f32[2,2,128]{2,1,0:T(2,128)S(1)} %slice_bitcast_fusion, ...), kind=kOutput, calls=%fused_computation.10 | convolution fusion | flops 16941056 | bytes 1329920 | tf_op jit(solution)/shard_map/mrkgs,mrskd->mrkgd/dot_general | solution.py:53
  59.4 13.1 %all_gather.3 = bf16[2,8,2048]{2,0,1:T(2,128)(2,1)S(1)} all-gather(bf16[2,2,2048]{2,0,1:T(2,128)(2,1)S(1)} %copy.12), channel_id=1, replica_groups=mesh['groups'=2,'gx'=4,'gy'=4] {'gx'}, dimensions={1}, use_global_device_ids=true | all-gather | bytes 81920 | tf_op jit(solution)/shard_map/all_gather | solution.py:83
  72.6 8.8 %fusion = f32[2,8,4096]{2,1,0:T(8,128)} fusion(bf16[2048,4096]{1,0:T(8,128)(2,1)} %param.12, bf16[2,8,2048]{2,0,1:T(2,128)(2,1)S(1)} %all_gather.3), kind=kOutput, calls=%fused_computation | convolution fusion | flops 268435456 | bytes 17104896 | tf_op jit(solution)/shard_map/mrc,cd->mrd/dot_general | solution.py:81
  81.3 0.0 all-reduce.7.cloned.1.call-update
  81.3 32.2 %all-reduce.7.cloned.1.call-done = f32[2,8,4096]{2,1,0:T(8,128)} async-done(((f32[2,8,4096]{2,1,0:T(8,128)}), f32[2,8,4096]{2,1,0:T(8,128)}) %all-reduce.7.cloned.1.call-update) | async-done | bytes 262160 | tf_op jit(solution)/shard_map/psum | solution.py:87
  113.5 1.6 %fusion.14 = bf16[2,8,4096]{2,1,0:T(8,128)(2,1)} fusion(f32[2,8,4096]{2,1,0:T(8,128)} %all-reduce.7.cloned.1.call-done, bf16[2,8,4096]{2,1,0:T(8,128)(2,1)S(1)} %copy-done.1), kind=kLoop, calls=%fused_computation.19 | loop fusion | flops 196608 | bytes 524288 | tf_op jit(solution)/shard_map/convert_element_type | solution.py:88
  (8 shorter events, 0.1 us)
Async XLA Ops:
  6.5 10.0 %copy-start = (bf16[4096,1,256]{2,0,1:T(8,128)(2,1)S(1)}, bf16[4096,1,256]{2,0,1:T(8,128)(2,1)}, u32[]{:S(2)}) copy-start(bf16[4096,1,256]{2,0,1:T(8,128)(2,1)} %param.11) | copy-start | bytes 6291460
  6.5 47.3 %all-reduce.9.cloned.1.call-start = ((), (), s32[]{:S(2)}) async-start(), calls=%async_computation.1 | async-start | bytes 262144
  7.4 8.9 %copy-start.1 = (bf16[2,8,4096]{2,1,0:T(8,128)(2,1)S(1)}, bf16[2,8,4096]{2,1,0:T(8,128)(2,1)}, u32[]{:S(2)}) copy-start(bf16[2,8,4096]{2,1,0:T(8,128)(2,1)} %param.7) | copy-start | bytes 393220
  7.4 9.0 %copy-start.2 = (s32[2,2]{1,0:T(2,128)S(1)}, s32[2,2]{1,0:T(2,128)}, u32[]{:S(2)}) copy-start(s32[2,2]{1,0:T(2,128)} %param.8) | copy-start | bytes 52
  16.2 0.7 copy-start.3
  16.2 97.3 %all-reduce.7.cloned.1.call-start = ((), (), s32[]{:S(2)}) async-start(), calls=%async_computation | async-start | bytes 524288 | tf_op jit(solution)/shard_map/psum | solution.py:87
Sparse Core Ops, SparseCore 0:
  16.4 37.4 all-reduce.8
  81.5 31.9 all-reduce.6
where the time goes:
time: 122 us
  waiting for transfers between devices  39.5 us (32%)
  blocking collectives  33.9 us (28%)
  matrix products  22 us (18%)
  between operations  14.2 us (12%)
  local copies, waits for them, and re-layouts  8.61 us (7%)
  other arithmetic  3.71 us (3%)
    psum x1, waiting for transfers between devices, local(): summed_heads = lax.psum(projected, 'gy')  32.2 us
    unnamed x1, blocking collectives  20.8 us
    all_gather x1, blocking collectives, local(): lax.all_gather(attended, 'gx', axis=1, tiled=True)  13.1 us
    dot_general x1, matrix products, local(): jnp.einsum('mrd,dc->mrc', normed, w_query, preferred_element_type=jnp.flo...  8.81 us
    dot_general x1, matrix products, local(): jnp.einsum('mrc,cd->mrd', lax.all_gather(attended, 'gx', axis=1, tiled=Tr...  8.75 us
    unnamed x3, waiting for transfers between devices  7.38 us
    slice x1, local copies, waits for them, and re-layouts, attend(): keys = cache[:, :, :, :, 0, :]  6.95 us
  transfers between devices with their start and end apart: 2, of which 2 were waited for; matrix products, arithmetic and copies ran while one was open for 7% of the time, Pallas kernels for 0%

commit v1 on v0

--- a/solution.py
+++ b/solution.py
@@ -5,6 +5,29 @@
 
 MODEL_WIDTH = 16384
 HEAD_SIZE = 128
+
+
+def _state_cells(point, pos_dim):
+    point = jnp.moveaxis(point, 0, pos_dim)
+    near = point.shape
+    field_out = point.reshape(
+        *near[:pos_dim], near[pos_dim] * near[pos_dim + 1], *near[pos_dim + 2 :]
+    )
+    return field_out
+
+
+def _name_positions(z, mesh_name, row_dim, mine, dim_k):
+    everything, y, newest = (lax.axis_size(mesh_name), lax.axis_index(mesh_name), z.shape[row_dim])
+    vals = [(hop_no, (hop_no + 1) % everything) for hop_no in range(everything)]
+    column = []
+    lower = z
+    for i in range(everything):
+        vec_out = lower if i == everything - 1 else lax.ppermute(lower, mesh_name, vals)
+        column.append(mine(lower, (y - i) % everything * newest))
+        lower = vec_out
+    column = jnp.stack(column)[(y - jnp.arange(everything)) % everything]
+    r1 = _state_cells(column, dim_k)
+    return r1
 
 
 def rotate(vectors, positions):
@@ -78,11 +101,14 @@
         lax.psum_scatter(squares, "gx", scatter_dimension=1, tiled=True),
     )
     attended = attend(query_sum, keyval_sum, local_squares, lengths, cache)
-    projected = jnp.einsum(
-        "mrc,cd->mrd",
-        lax.all_gather(attended, "gx", axis=1, tiled=True),
-        w_out,
-        preferred_element_type=jnp.float32,
+    projected = _name_positions(
+        attended,
+        "gx",
+        1,
+        lambda shard, start: jnp.einsum(
+            "mrc,cd->mrd", shard, w_out, preferred_element_type=jnp.float32
+        ),
+        1,
     )
     summed_heads = lax.psum(projected, "gy")
     return (x_full + summed_heads).astype(jnp.bfloat16)

time: 122 us -> 130 us (1.066)
  matrix products: 22 us -> 35.7 us
  blocking collectives: 33.9 us -> 21.2 us
  starting transfers between devices: 0.04 us -> 3.07 us
  local copies, waits for them, and re-layouts: 8.61 us -> 10.4 us
  waiting for transfers between devices: 39.5 us -> 41.1 us
    dot_general x1 -> x4, matrix products: 8.75 us -> 22.5 us  [local(): jnp.einsum('mrc,cd->mrd', shard, w_out, preferred_element_type=jnp.float32)]
    all_gather x1 -> x0, blocking collectives: 13.1 us -> none  [local(): lax.all_gather(attended, 'gx', axis=1, tiled=True)]
    ppermute x0 -> x3, waiting for transfers between devices: none -> 3.03 us  [_name_positions(): lax.ppermute(lower, mesh_name, vals)]
    ppermute x0 -> x3, starting transfers between devices: none -> 3 us  [_name_positions(): lax.ppermute(lower, mesh_name, vals)]
  transfers between devices with their start and end apart: 2 -> 5, of which waited for: 2 -> 3; matrix products, arithmetic and copies ran while one was open for 7% -> 22% of each run, Pallas kernels for 0% -> 0%
where the time goes in v1:
time: 130 us; the launch traced here: 129 us
  waiting for transfers between devices  41.1 us (32%)
  matrix products  35.7 us (27%)
  blocking collectives  21.2 us (16%)
  between operations  14.2 us (11%)
  local copies, waits for them, and re-layouts  10.4 us (8%)
  other arithmetic  3.86 us (3%)
  starting transfers between devices  3.07 us (2%)
    psum x1, waiting for transfers between devices, local(): summed_heads = lax.psum(projected, 'gy')  30.9 us
    dot_general x4, matrix products, local(): jnp.einsum('mrc,cd->mrd', shard, w_out, preferred_element_type=jnp.float32)  22.5 us
    unnamed x1, blocking collectives  21.2 us
    dot_general x1, matrix products, local(): jnp.einsum('mrd,dc->mrc', normed, w_query, preferred_element_type=jnp.flo...  8.78 us
    unnamed x3, waiting for transfers between devices  7.13 us
    slice x1, local copies, waits for them, and re-layouts, attend(): keys = cache[:, :, :, :, 0, :]  6.89 us
    ppermute x3, waiting for transfers between devices, _name_positions(): lax.ppermute(lower, mesh_name, vals)  3.03 us
    ppermute x3, starting transfers between devices, _name_positions(): lax.ppermute(lower, mesh_name, vals)  3 us
  transfers between devices with their start and end apart: 5, of which 3 were waited for; matrix products, arithmetic and copies ran while one was open for 22% of the time, Pallas kernels for 0%

profile of v1, /device:TPU:0, one launch (start us, length us, event | category | flops | bytes accessed | tf_op | source)
XLA Modules:
  0.0 129.4 jit_solution(12856610856104826365)
XLA Ops:
  6.5 0.0 copy-start
  6.5 0.0 copy-start.3
  6.5 0.0 copy-start.1
  6.5 0.0 copy-start.2
  6.5 0.0 all-reduce.9.cloned.1.call-start
  6.6 0.8 convert_element_type.46
  7.4 8.8 %fusion.8 = f32[2,8,2048]{2,1,0:T(8,128)} fusion(bf16[4096,2048]{1,0:T(8,128)(2,1)} %param.10, bf16[2,8,4096]{2,1,0:T(8,128)(2,1)} %param.7, f32[4096]{0:T(1024)S(1)} %convert_element_type.46), kind=kOutput, calls=%fused_computation.9 | convolution fusion | flops 268632064 | bytes 17055744 | tf_op jit(solution)/shard_map/mrd,dc->mrc/dot_general | solution.py:94
  16.2 0.0 all-reduce.9.cloned.1.call-update
  16.2 0.0 all-reduce.7.cloned.1.call-start
  16.3 0.0 copy-done.1
  16.3 0.1 fusion.31
  16.4 0.0 copy-done.2
  16.4 0.1 iota_compare_fusion
  16.5 0.0 copy-done
  16.5 0.4 fusion.27
  16.9 21.2 %all-reduce.3 = (f32[2,8]{1,0:T(2,128)S(1)}, f32[2,8,1,256]{3,1,0,2:T(8,128)S(1)}) all-reduce(f32[2,8]{1,0:T(2,128)S(1)} %fusion.31, f32[2,8,1,256]{3,1,0,2:T(8,128)S(1)} %fusion.27), channel_id=3, replica_groups=mesh['groups'=2,'gx'=4,'gy'=4] {'gx'}, use_global_device_ids=true, to_apply=%region_2.0.clone | all-reduce | flops 4112 | bytes 32896
  38.1 0.0 copy-done.3
  38.1 0.6 dynamic-slice
  39.3 0.1 fusion.49
  39.4 0.1 dynamic-slice_multiply_fusion
  39.4 0.1 multiply_cosine_fusion.1
  39.6 0.1 fusion.46
  39.7 6.9 %fusion.54 = (bf16[2,2,1024,1,1,128]{5,4,3,2,1,0:T(2,128)(2,1)}, bf16[2,2,1024,1,1,128]{5,4,3,2,1,0:T(2,128)(2,1)}) fusion(bf16[2,2,1024,1,2,128]{5,4,3,2,1,0:T(2,128)(2,1)} %param.13), kind=kLoop, calls=%fused_computation.73 | loop fusion | bytes 4194304 | tf_op jit(solution)/shard_map/slice | solution.py:61
  46.6 0.1 maximum_bitcast_fusion
  46.7 7.1 %all-reduce.9.cloned.1.call-done = f32[2,8,2048]{2,1,0:T(8,128)} async-done(((f32[2,8,2048]{2,1,0:T(8,128)}), f32[2,8,2048]{2,1,0:T(8,128)}) %all-reduce.9.cloned.1.call-update) | async-done | bytes 131088
  53.8 0.9 constant_dynamic-slice_fusion
  54.7 0.1 broadcast_multiply_fusion
  54.8 0.1 subtract_convert_fusion
  54.9 0.2 multiply_reduce_fusion
  55.1 2.1 %fusion.55 = (f32[2,2,16]{2,1,0:T(2,128)S(1)}, f32[2,2,16,1024]{3,2,1,0:T(8,128)S(1)}) fusion(bf16[2,2,1024,1,1,128]{5,4,3,2,1,0:T(2,128)(2,1)} %get-tuple-element.9, bf16[2,2,16,64]{3,2,1,0:T(8,128)(2,1)S(1)} %bitcast.72, bf16[2,2,16,64]{3,2,1,0:T(8,128)(2,1)S(1)} %bitcast.71, pred[2,2,1024]{2,1,0:T(4,128)(4,1)S(1)} %iota_compare_fusion), kind=kOutput, calls=%fused_computation.74 | convolution fusion | flops 17006528 | bytes 1331456 | tf_op jit(solution)/shard_map/mrkgd,mrskd->mrkgs/dot_general | solution.py:64
  57.2 0.2 fusion.33
  57.4 1.9 %fusion.26 = bf16[2,2,16,128]{3,2,1,0:T(8,128)(2,1)S(1)} fusion(bf16[2,2,1024,1,1,128]{5,4,3,2,1,0:T(2,128)(2,1)} %get-tuple-element.10, f32[2,2,16,1024]{3,2,1,0:T(8,128)S(1)} %get-tuple-element.18, f32[2,2,16]{2,1,0:T(2,128)S(1)} %multiply_maximum_fusion, f32[2,2,16]{2,1,0:T(2,128)S(1)} %get-tuple-element.7, f32[2,2,128]{2,1,0:T(2,128)S(1)} %slice_bitcast_fusion, ...), kind=kOutput, calls=%fused_computation.21 | convolution fusion | flops 16941056 | bytes 1329920 | tf_op jit(solution)/shard_map/mrkgs,mrskd->mrkgd/dot_general | solution.py:76
  59.3 0.0 slice-start
  59.4 0.0 slice-start.1
  59.4 1.5 %collective-permute-start = (bf16[2,2,2048]{2,1,0:T(2,128)(2,1)S(1)}, bf16[2,2,2048]{2,1,0:T(2,128)(2,1)S(1)}, u32[]{:S(2)}, u32[]{:S(2)}) collective-permute-start(bf16[2,2,2048]{2,1,0:T(2,128)(2,1)S(1)} %reshape.251), channel_id=1, source_target_pairs={{0,4},{4,8},{8,12},{12,0},{1,5},{5,9},{9,13},{13,1},{2,6},{6,10},{... | collective-permute-start | bytes 49160 | tf_op jit(solution)/shard_map/ppermute | solution.py:25
  60.8 8.8 %fusion.10 = f32[1,2,2,4096]{3,2,1,0:T(2,128)S(1)} fusion(bf16[2,2,2048]{2,1,0:T(2,128)(2,1)S(1)} %reshape.251, bf16[2048,4096]{1,0:T(8,128)(2,1)} %param.12), kind=kOutput, calls=%fused_computation.11 | convolution fusion | flops 67108864 | bytes 16859136 | tf_op jit(solution)/shard_map/mrc,cd->mrd/dot_general | solution.py:108
  69.6 0.0 slice-start.2
  69.7 0.0 slice-start.3
  69.7 0.0 collective-permute-done
  69.7 1.3 collective-permute-start.1
  71.0 8.8 %fusion.13 = f32[1,2,2,4096]{3,2,1,0:T(2,128)S(1)} fusion(bf16[2,2,2048]{2,1,0:T(2,128)(2,1)S(1)} %collective-permute-done, bf16[2048,4096]{1,0:T(8,128)(2,1)} %param.12), kind=kOutput, calls=%fused_computation.12 | convolution fusion | flops 67108864 | bytes 16859136 | tf_op jit(solution)/shard_map/mrc,cd->mrd/dot_general | solution.py:108
  79.7 0.0 collective-permute-done.1
  79.7 0.3 collective-permute-start.2
  80.0 0.0 slice-done
  80.0 0.0 slice-done.1
  80.0 0.0 slice-done.2
  80.0 0.0 slice-done.3
  80.0 2.5 %fusion.16 = f32[1,2,2,4096]{3,2,1,0:T(2,128)S(1)} fusion(bf16[2,2,2048]{2,1,0:T(2,128)(2,1)S(1)} %collective-permute-done.1, bf16[2048,4096]{1,0:T(8,128)(2,1)S(1)} %bitcast.68), kind=kOutput, calls=%fused_computation.13 | convolution fusion | flops 67108864 | bytes 16859136 | tf_op jit(solution)/shard_map/mrc,cd->mrd/dot_general | solution.py:108
  82.5 3.0 %collective-permute-done.2 = bf16[2,2,2048]{2,1,0:T(2,128)(2,1)S(1)} collective-permute-done((bf16[2,2,2048]{2,1,0:T(2,128)(2,1)S(1)}, bf16[2,2,2048]{2,1,0:T(2,128)(2,1)S(1)}, u32[]{:S(2)}, u32[]{:S(2)}) %collective-permute-start.2) | collective-permute-done | bytes 16416 | tf_op jit(solution)/shard_map/ppermute | solution.py:25
  85.5 2.5 %fusion.19 = f32[1,2,2,4096]{3,2,1,0:T(2,128)S(1)} fusion(bf16[2,2,2048]{2,1,0:T(2,128)(2,1)S(1)} %collective-permute-done.2, bf16[2048,4096]{1,0:T(8,128)(2,1)S(1)} %bitcast.68), kind=kOutput, calls=%fused_computation.14 | convolution fusion | flops 67108864 | bytes 16859136 | tf_op jit(solution)/shard_map/mrc,cd->mrd/dot_general | solution.py:108
  88.0 0.1 pad_maximum_fusion
  88.1 0.8 gather_fusion
  88.9 0.2 copy.29
  89.2 0.9 copy.30
  90.0 0.0 all-reduce.7.cloned.1.call-update
  90.0 30.9 %all-reduce.7.cloned.1.call-done = f32[2,8,4096]{2,1,0:T(8,128)} async-done(((f32[2,8,4096]{2,1,0:T(8,128)}), f32[2,8,4096]{2,1,0:T(8,128)}) %all-reduce.7.cloned.1.call-update) | async-done | bytes 262160 | tf_op jit(solution)/shard_map/psum | solution.py:113
  120.9 1.6 %fusion.32 = bf16[2,8,4096]{2,1,0:T(8,128)(2,1)} fusion(f32[2,8,4096]{2,1,0:T(8,128)} %all-reduce.7.cloned.1.call-done, bf16[2,8,4096]{2,1,0:T(8,128)(2,1)S(1)} %copy-done.1), kind=kLoop, calls=%fused_computation.30 | loop fusion | flops 196608 | bytes 524288 | tf_op jit(solution)/shard_map/convert_element_type | solution.py:114
  (10 shorter events, 0.1 us)
Async XLA Ops:
  6.5 10.0 %copy-start = (bf16[4096,1,256]{2,0,1:T(8,128)(2,1)S(1)}, bf16[4096,1,256]{2,0,1:T(8,128)(2,1)}, u32[]{:S(2)}) copy-start(bf16[4096,1,256]{2,0,1:T(8,128)(2,1)} %param.11) | copy-start | bytes 6291460
  6.5 31.6 %copy-start.3 = (u32[32]{0:T(128)S(1)}, u32[32]{0:T(128)}, u32[]{:S(2)}) copy-start(u32[32]{0:T(128)} %constant.49) | copy-start | bytes 388
  6.5 9.7 %copy-start.1 = (bf16[2,8,4096]{2,1,0:T(8,128)(2,1)S(1)}, bf16[2,8,4096]{2,1,0:T(8,128)(2,1)}, u32[]{:S(2)}) copy-start(bf16[2,8,4096]{2,1,0:T(8,128)(2,1)} %param.7) | copy-start | bytes 393220
  6.5 9.9 %copy-start.2 = (s32[2,2]{1,0:T(2,128)S(1)}, s32[2,2]{1,0:T(2,128)}, u32[]{:S(2)}) copy-start(s32[2,2]{1,0:T(2,128)} %param.8) | copy-start | bytes 52
  6.5 47.2 %all-reduce.9.cloned.1.call-start = ((), (), s32[]{:S(2)}) async-start(), calls=%async_computation.1 | async-start | bytes 262144
  16.2 104.7 %all-reduce.7.cloned.1.call-start = ((), (), s32[]{:S(2)}) async-start(), calls=%async_computation | async-start | bytes 524288 | tf_op jit(solution)/shard_map/psum | solution.py:113
  59.3 20.7 %slice-start = ((s8[16777216]{0:T(1024)(128)(4,1)}), s8[4194304]{0:T(1024)(128)(4,1)S(1)}, s32[]{:S(2)}) async-start(s8[16777216]{0:T(1024)(128)(4,1)} %bitcast.67), calls=%async_computation.2 | async-start | bytes 8388608
  59.4 20.7 %slice-start.1 = ((s8[16777216]{0:T(1024)(128)(4,1)}), s8[4194304]{0:T(1024)(128)(4,1)S(1)}, s32[]{:S(2)}) async-start(s8[16777216]{0:T(1024)(128)(4,1)} %bitcast.67), calls=%async_computation.3 | async-start | bytes 8388608
  59.4 10.3 %collective-permute-start = (bf16[2,2,2048]{2,1,0:T(2,128)(2,1)S(1)}, bf16[2,2,2048]{2,1,0:T(2,128)(2,1)S(1)}, u32[]{:S(2)}, u32[]{:S(2)}) collective-permute-start(bf16[2,2,2048]{2,1,0:T(2,128)(2,1)S(1)} %reshape.251), channel_id=1, source_target_pairs={{0,4},{4,8},{8,12},{12,0},{1,5},{5,9},{9,13},{13,1},{2,6},{6,10},{... | collective-permute-start | bytes 49160 | tf_op jit(solution)/shard_map/ppermute | solution.py:25
  69.6 10.4 %slice-start.2 = ((s8[16777216]{0:T(1024)(128)(4,1)}), s8[4194304]{0:T(1024)(128)(4,1)S(1)}, s32[]{:S(2)}) async-start(s8[16777216]{0:T(1024)(128)(4,1)} %bitcast.67), calls=%async_computation.4 | async-start | bytes 8388608
  69.7 10.4 %slice-start.3 = ((s8[16777216]{0:T(1024)(128)(4,1)}), s8[4194304]{0:T(1024)(128)(4,1)S(1)}, s32[]{:S(2)}) async-start(s8[16777216]{0:T(1024)(128)(4,1)} %bitcast.67), calls=%async_computation.5 | async-start | bytes 8388608
  69.7 10.0 %collective-permute-start.1 = (bf16[2,2,2048]{2,1,0:T(2,128)(2,1)S(1)}, bf16[2,2,2048]{2,1,0:T(2,128)(2,1)S(1)}, u32[]{:S(2)}, u32[]{:S(2)}) collective-permute-start(bf16[2,2,2048]{2,1,0:T(2,128)(2,1)S(1)} %collective-permute-done), channel_id=1, source_target_pairs={{0,4},{4,8},{8,12},{12,0},{1,5},{5,9},{9,13},{13,1},{2,6},{6,10},{... | collective-permute-start | bytes 49160 | tf_op jit(solution)/shard_map/ppermute | solution.py:25
  79.7 5.8 %collective-permute-start.2 = (bf16[2,2,2048]{2,1,0:T(2,128)(2,1)S(1)}, bf16[2,2,2048]{2,1,0:T(2,128)(2,1)S(1)}, u32[]{:S(2)}, u32[]{:S(2)}) collective-permute-start(bf16[2,2,2048]{2,1,0:T(2,128)(2,1)S(1)} %collective-permute-done.1), channel_id=1, source_target_pairs={{0,4},{4,8},{8,12},{12,0},{1,5},{5,9},{9,13},{13,1},{2,6},{6,10},{... | collective-permute-start | bytes 49160 | tf_op jit(solution)/shard_map/ppermute | solution.py:25
Sparse Core Ops, SparseCore 0:
  16.4 37.3 all-reduce.8
  90.1 30.7 all-reduce.6
